TPU v7x, 256 devices: a whole 4x4x8 slice. The times are simulated.
256 devices in a mesh: span: 256 (over x, y, z, core).
Axes of the slice: x: 4, y: 4, z: 8, core: 2. Of those that a mesh axis runs over, the one named last changes fastest.
Arguments:
- random_slabs: bfloat16 [8192, 4, 3, 2048], P('span'), may hold values from -6 to 6
- span_weights: float32 [513], replicated, may hold values from 0.1 to 2
- wall_filter: bfloat16 [2048, 2048], replicated, may hold values from -0.125 to 0.125
- prev_state: float32 [8192, 3, 2048], P('span'), may hold values from -6 to 6
- time_scale: float32 [3, 2048], replicated, may hold values from 1 to 32
- mean_velocity: float32 [2048], replicated, may hold values from 0 to 2
- lund_diag: float32 [3, 2048], replicated, may hold values from 0.3 to 3
- lund_off: float32 [3, 2048], replicated, may hold values from -1 to 1
Outputs:
- velocity: bfloat16 [8192, 4, 3, 2048], P('span')
- new_state: float32 [8192, 3, 2048], P('span')
All inputs are finite; a program needn't handle non-finite values.
Results may differ from a plain program's by a relative error of at most 0.0051.
Values may be sent and summed in bfloat16 or wider, within the bound.
A program may use at most 128 MiB of HBM per device.

v0:
```python
import jax
import jax.numpy as jnp
from jax import lax
from jax.sharding import PartitionSpec as P


def from_behind(value, axis, by):
    count = lax.axis_size(axis)
    return lax.ppermute(value, axis, [(i, (i + by) % count) for i in range(count)])


def band_matrix(taps, height):
    reach = taps.shape[0]
    padded = jnp.concatenate([taps, jnp.zeros((height,), taps.dtype)])
    length = reach + height
    tiled = jnp.tile(padded, height)[: height * (length - 1)]
    return tiled.reshape(height, length - 1)


def tap_block(matrix, rows, distance):
    return matrix[:, (8 + distance) * rows : (9 + distance) * rows]


def body(
    random_slabs,
    span_weights,
    wall_filter,
    prev_state,
    time_scale,
    mean_velocity,
    lund_diag,
    lund_off,
):
    rows = random_slabs.shape[0]
    planes = random_slabs.shape[1]
    width = random_slabs.shape[3]
    columns = planes * 3 * width
    flat = random_slabs.reshape(rows, columns)
    scaling = jnp.sqrt(jnp.sum(span_weights * span_weights))
    taps = (span_weights / scaling).astype(jnp.bfloat16)
    matrix = band_matrix(taps, rows)
    summed = jnp.dot(tap_block(matrix, rows, 0), flat, preferred_element_type=jnp.float32)
    below = flat
    above = flat
    for distance in range(1, 9):
        below = from_behind(below, "span", 1)
        summed = summed + jnp.dot(
            tap_block(matrix, rows, -distance), below, preferred_element_type=jnp.float32
        )
        above = from_behind(above, "span", -1)
        summed = summed + jnp.dot(
            tap_block(matrix, rows, distance), above, preferred_element_type=jnp.float32
        )
    spanned = summed.astype(jnp.bfloat16).reshape(rows, planes, 3, width)
    filtered = lax.dot_general(
        spanned, wall_filter, (((3,), (1,)), ((), ())), preferred_element_type=jnp.float32
    )
    decay = jnp.exp(-jnp.pi / (2.0 * time_scale))
    inject = jnp.sqrt(1.0 - jnp.exp(-jnp.pi / time_scale))
    state = prev_state
    outputs = []
    for plane in range(planes):
        state = decay * state + inject * filtered[:, plane]
        along = state[:, 0]
        normal = state[:, 1]
        spanwise = state[:, 2]
        first = mean_velocity + lund_diag[0] * along
        second = lund_off[0] * along + lund_diag[1] * normal
        third = lund_off[1] * along + lund_off[2] * normal + lund_diag[2] * spanwise
        outputs.append(jnp.stack([first, second, third], axis=1).astype(jnp.bfloat16))
    velocity = jnp.stack(outputs, axis=1)
    return (velocity, state)


def solution(mesh):
    placed = (P("span", None, None, None), P(), P(), P("span", None, None), P(), P(), P(), P())
    return jax.shard_map(
        body,
        mesh=mesh,
        in_specs=placed,
        out_specs=(P("span", None, None, None), P("span", None, None)),
        check_vma=False,
    )
```

profile of v0, /device:TPU:0, one launch (start us, length us, event | category | flops | bytes accessed | tf_op | source)
XLA Modules:
  0.0 236.0 jit_solution(18219296884152110191)
XLA Ops:
  0.6 2.9 %copy.12 = bf16[32,4,3,2048]{3,2,1,0:T(4,128)(2,1)S(1)} copy(bf16[32,4,3,2048]{3,1,2,0:T(4,128)(2,1)} %param.8) | data formatting | bytes 3145728 | tf_op args[0]
  3.5 0.0 copy-start.12
  3.5 0.0 copy-start.11
  3.5 0.0 copy-start.13
  3.6 0.0 copy-start.14
  3.6 3.2 %reshape.359 = bf16[32,24576]{1,0:T(8,128)(2,1)} reshape(bf16[32,4,3,2048]{3,2,1,0:T(4,128)(2,1)S(1)} %copy.12) | data formatting | bytes 3145728 | tf_op jit(solution)/shard_map/reshape | solution.py:38
  6.7 8.2 %collective-permute-start.1 = (bf16[32,24576]{1,0:T(8,128)(2,1)}, bf16[32,24576]{1,0:T(8,128)(2,1)S(1)}, u32[]{:S(2)}, u32[]{:S(2)}) collective-permute-start(bf16[32,24576]{1,0:T(8,128)(2,1)} %reshape.359), channel_id=1, source_target_pairs={{0,255},{1,0},{2,1},{3,2},{4,3},{5,4},{6,5},{7,6},{8,7},{9,8},{10,... | collective-permute-start | bytes 4718600 | tf_op jit(solution)/shard_map/ppermute | solution.py:9
  15.0 18.2 %collective-permute-done.1 = bf16[32,24576]{1,0:T(8,128)(2,1)S(1)} collective-permute-done((bf16[32,24576]{1,0:T(8,128)(2,1)}, bf16[32,24576]{1,0:T(8,128)(2,1)S(1)}, u32[]{:S(2)}, u32[]{:S(2)}) %collective-permute-start.1) | collective-permute-done | bytes 1572896 | tf_op jit(solution)/shard_map/ppermute | solution.py:9
  33.2 7.2 %collective-permute-start.3 = (bf16[32,24576]{1,0:T(8,128)(2,1)S(1)}, bf16[32,24576]{1,0:T(8,128)(2,1)S(1)}, u32[]{:S(2)}, u32[]{:S(2)}) collective-permute-start(bf16[32,24576]{1,0:T(8,128)(2,1)S(1)} %collective-permute-done.1), channel_id=1, source_target_pairs={{0,255},{1,0},{2,1},{3,2},{4,3},{5,4},{6,5},{7,6},{8,7},{9,8},{10,... | collective-permute-start | bytes 4718600 | tf_op jit(solution)/shard_map/ppermute | solution.py:9
  40.5 17.9 %collective-permute-done.3 = bf16[32,24576]{1,0:T(8,128)(2,1)S(1)} collective-permute-done((bf16[32,24576]{1,0:T(8,128)(2,1)S(1)}, bf16[32,24576]{1,0:T(8,128)(2,1)S(1)}, u32[]{:S(2)}, u32[]{:S(2)}) %collective-permute-start.3) | collective-permute-done | bytes 1572896 | tf_op jit(solution)/shard_map/ppermute | solution.py:9
  58.4 7.3 %collective-permute-start.5 = (bf16[32,24576]{1,0:T(8,128)(2,1)S(1)}, bf16[32,24576]{1,0:T(8,128)(2,1)S(1)}, u32[]{:S(2)}, u32[]{:S(2)}) collective-permute-start(bf16[32,24576]{1,0:T(8,128)(2,1)S(1)} %collective-permute-done.3), channel_id=1, source_target_pairs={{0,255},{1,0},{2,1},{3,2},{4,3},{5,4},{6,5},{7,6},{8,7},{9,8},{10,... | collective-permute-start | bytes 4718600 | tf_op jit(solution)/shard_map/ppermute | solution.py:9
  65.7 0.0 collective-permute-done.2
  65.7 17.9 %collective-permute-done.5 = bf16[32,24576]{1,0:T(8,128)(2,1)S(1)} collective-permute-done((bf16[32,24576]{1,0:T(8,128)(2,1)S(1)}, bf16[32,24576]{1,0:T(8,128)(2,1)S(1)}, u32[]{:S(2)}, u32[]{:S(2)}) %collective-permute-start.5) | collective-permute-done | bytes 1572896 | tf_op jit(solution)/shard_map/ppermute | solution.py:9
  83.7 7.3 %collective-permute-start.7 = (bf16[32,24576]{1,0:T(8,128)(2,1)S(1)}, bf16[32,24576]{1,0:T(8,128)(2,1)}, u32[]{:S(2)}, u32[]{:S(2)}) collective-permute-start(bf16[32,24576]{1,0:T(8,128)(2,1)S(1)} %collective-permute-done.5), channel_id=1, source_target_pairs={{0,255},{1,0},{2,1},{3,2},{4,3},{5,4},{6,5},{7,6},{8,7},{9,8},{10,... | collective-permute-start | bytes 4718600 | tf_op jit(solution)/shard_map/ppermute | solution.py:9
  91.0 0.1 collective-permute-done.4
  91.1 0.1 collective-permute-start.6
  91.3 0.1 divide_exponential_fusion
  91.3 17.6 %collective-permute-done.7 = bf16[32,24576]{1,0:T(8,128)(2,1)} collective-permute-done((bf16[32,24576]{1,0:T(8,128)(2,1)S(1)}, bf16[32,24576]{1,0:T(8,128)(2,1)}, u32[]{:S(2)}, u32[]{:S(2)}) %collective-permute-start.7) | collective-permute-done | bytes 1572896 | tf_op jit(solution)/shard_map/ppermute | solution.py:9
  108.9 7.4 %collective-permute-start.9 = (bf16[32,24576]{1,0:T(8,128)(2,1)}, bf16[32,24576]{1,0:T(8,128)(2,1)}, u32[]{:S(2)}, u32[]{:S(2)}) collective-permute-start(bf16[32,24576]{1,0:T(8,128)(2,1)} %collective-permute-done.7), channel_id=1, source_target_pairs={{0,255},{1,0},{2,1},{3,2},{4,3},{5,4},{6,5},{7,6},{8,7},{9,8},{10,... | collective-permute-start | bytes 4718600 | tf_op jit(solution)/shard_map/ppermute | solution.py:9
  116.4 0.6 multiply_reduce_fusion
  117.7 0.1 collective-permute-start.8
  117.9 0.1 tile.10
  118.0 0.1 reshape.358
  118.2 2.1 fusion.62
  120.2 0.6 convolution_add_fusion.8
  120.9 0.8 copy-done.2
  121.7 0.7 convolution_add_fusion.7
  122.3 12.3 %collective-permute-done.9 = bf16[32,24576]{1,0:T(8,128)(2,1)} collective-permute-done((bf16[32,24576]{1,0:T(8,128)(2,1)}, bf16[32,24576]{1,0:T(8,128)(2,1)}, u32[]{:S(2)}, u32[]{:S(2)}) %collective-permute-start.9) | collective-permute-done | bytes 1572896 | tf_op jit(solution)/shard_map/ppermute | solution.py:9
  134.6 7.3 %collective-permute-start.11 = (bf16[32,24576]{1,0:T(8,128)(2,1)}, bf16[32,24576]{1,0:T(8,128)(2,1)S(1)}, u32[]{:S(2)}, u32[]{:S(2)}) collective-permute-start(bf16[32,24576]{1,0:T(8,128)(2,1)} %collective-permute-done.9), channel_id=1, source_target_pairs={{0,255},{1,0},{2,1},{3,2},{4,3},{5,4},{6,5},{7,6},{8,7},{9,8},{10,... | collective-permute-start | bytes 4718600 | tf_op jit(solution)/shard_map/ppermute | solution.py:9
  142.0 0.6 fusion.57
  142.6 0.6 collective-permute-done.8
  143.2 0.7 fusion.6
  143.9 0.2 copy-done.6
  144.0 0.6 fusion.54
  144.6 2.1 fusion.5
  146.7 13.5 %collective-permute-done.11 = bf16[32,24576]{1,0:T(8,128)(2,1)S(1)} collective-permute-done((bf16[32,24576]{1,0:T(8,128)(2,1)}, bf16[32,24576]{1,0:T(8,128)(2,1)S(1)}, u32[]{:S(2)}, u32[]{:S(2)}) %collective-permute-start.11) | collective-permute-done | bytes 1572896 | tf_op jit(solution)/shard_map/ppermute | solution.py:9
  160.2 7.2 %collective-permute-start.13 = (bf16[32,24576]{1,0:T(8,128)(2,1)S(1)}, bf16[32,24576]{1,0:T(8,128)(2,1)S(1)}, u32[]{:S(2)}, u32[]{:S(2)}) collective-permute-start(bf16[32,24576]{1,0:T(8,128)(2,1)S(1)} %collective-permute-done.11), channel_id=1, source_target_pairs={{0,255},{1,0},{2,1},{3,2},{4,3},{5,4},{6,5},{7,6},{8,7},{9,8},{10,... | collective-permute-start | bytes 4718600 | tf_op jit(solution)/shard_map/ppermute | solution.py:9
  167.5 2.0 fusion.51
  169.4 0.1 collective-permute-start.12
  169.5 0.6 fusion.4
  170.2 2.1 fusion.48
  172.2 2.1 fusion.3
  174.3 11.1 %collective-permute-done.13 = bf16[32,24576]{1,0:T(8,128)(2,1)S(1)} collective-permute-done((bf16[32,24576]{1,0:T(8,128)(2,1)S(1)}, bf16[32,24576]{1,0:T(8,128)(2,1)S(1)}, u32[]{:S(2)}, u32[]{:S(2)}) %collective-permute-start.13) | collective-permute-done | bytes 1572896 | tf_op jit(solution)/shard_map/ppermute | solution.py:9
  185.4 7.3 %collective-permute-start.15 = (bf16[32,24576]{1,0:T(8,128)(2,1)S(1)}, bf16[32,24576]{1,0:T(8,128)(2,1)S(1)}, u32[]{:S(2)}, u32[]{:S(2)}) collective-permute-start(bf16[32,24576]{1,0:T(8,128)(2,1)S(1)} %collective-permute-done.13), channel_id=1, source_target_pairs={{0,255},{1,0},{2,1},{3,2},{4,3},{5,4},{6,5},{7,6},{8,7},{9,8},{10,... | collective-permute-start | bytes 4718600 | tf_op jit(solution)/shard_map/ppermute | solution.py:9
  192.7 0.6 fusion.45
  193.3 1.4 collective-permute-done.12
  194.8 0.6 fusion.2
  195.4 0.6 fusion.42
  196.0 0.6 fusion.1
  196.7 14.0 %collective-permute-done.15 = bf16[32,24576]{1,0:T(8,128)(2,1)S(1)} collective-permute-done((bf16[32,24576]{1,0:T(8,128)(2,1)S(1)}, bf16[32,24576]{1,0:T(8,128)(2,1)S(1)}, u32[]{:S(2)}, u32[]{:S(2)}) %collective-permute-start.15) | collective-permute-done | bytes 1572896 | tf_op jit(solution)/shard_map/ppermute | solution.py:9
  210.7 0.5 fusion.39
  211.2 8.8 %collective-permute-done.14 = bf16[32,24576]{1,0:T(8,128)(2,1)S(1)} collective-permute-done((bf16[32,24576]{1,0:T(8,128)(2,1)S(1)}, bf16[32,24576]{1,0:T(8,128)(2,1)S(1)}, u32[]{:S(2)}, u32[]{:S(2)}) %collective-permute-start.14) | collective-permute-done | bytes 1572896 | tf_op jit(solution)/shard_map/ppermute | solution.py:9
  220.0 0.6 fusion.7
  220.6 3.3 %reshape.360 = bf16[32,4,3,2048]{3,2,1,0:T(4,128)(2,1)} reshape(bf16[32,24576]{1,0:T(8,128)(2,1)S(1)} %fusion.7) | data formatting | bytes 3145728 | tf_op jit(solution)/shard_map/reshape | solution.py:54
  223.9 8.1 %fusion.8 = f32[32,4,3,2048]{3,0,2,1:T(8,128)S(1)} fusion(bf16[2048,2048]{1,0:T(8,128)(2,1)} %param.10, bf16[32,4,3,2048]{3,2,1,0:T(4,128)(2,1)} %reshape.360), kind=kOutput, calls=%fused_computation.17 | convolution fusion | flops 3221225472 | bytes 13107200 | tf_op jit(solution)/shard_map/dot_general | solution.py:55
  232.0 0.0 copy-start.10
  232.1 0.4 fusion.12
  232.5 0.0 copy-start
  232.5 0.2 copy-done.10
  232.7 0.2 fusion.31
  233.0 0.2 fusion.33
  233.2 0.1 copy-done
  233.4 0.2 maximum_maximum_fusion
  233.6 2.4 copy.14
  (34 shorter events, 0.1 us)
Async XLA Ops:
  3.5 87.7 %copy-start.12 = (f32[3,2048]{1,0:T(4,128)S(1)}, f32[3,2048]{1,0:T(4,128)}, u32[]{:S(2)}) copy-start(f32[3,2048]{1,0:T(4,128)} %param.14) | copy-start | bytes 73732
  3.5 87.7 %copy-start.11 = (f32[3,2048]{1,0:T(4,128)S(1)}, f32[3,2048]{1,0:T(4,128)}, u32[]{:S(2)}) copy-start(f32[3,2048]{1,0:T(4,128)} %param.12) | copy-start | bytes 73732
  3.5 112.8 %copy-start.13 = (f32[3,2048]{1,0:T(4,128)S(1)}, f32[3,2048]{1,0:T(4,128)}, u32[]{:S(2)}) copy-start(f32[3,2048]{1,0:T(4,128)} %param.15) | copy-start | bytes 73732
  3.6 112.9 %copy-start.14 = (f32[513]{0:T(1024)S(1)}, f32[513]{0:T(1024)}, u32[]{:S(2)}) copy-start(f32[513]{0:T(1024)} %param.9) | copy-start | bytes 6160
  6.7 26.5 %collective-permute-start.1 = (bf16[32,24576]{1,0:T(8,128)(2,1)}, bf16[32,24576]{1,0:T(8,128)(2,1)S(1)}, u32[]{:S(2)}, u32[]{:S(2)}) collective-permute-start(bf16[32,24576]{1,0:T(8,128)(2,1)} %reshape.359), channel_id=1, source_target_pairs={{0,255},{1,0},{2,1},{3,2},{4,3},{5,4},{6,5},{7,6},{8,7},{9,8},{10,... | collective-permute-start | bytes 4718600 | tf_op jit(solution)/shard_map/ppermute | solution.py:9
  15.0 25.5 %collective-permute-start = (bf16[32,24576]{1,0:T(8,128)(2,1)}, bf16[32,24576]{1,0:T(8,128)(2,1)S(1)}, u32[]{:S(2)}, u32[]{:S(2)}) collective-permute-start(bf16[32,24576]{1,0:T(8,128)(2,1)} %reshape.359), channel_id=1, source_target_pairs={{0,1},{1,2},{2,3},{3,4},{4,5},{5,6},{6,7},{7,8},{8,9},{9,10},{10,1... | collective-permute-start | bytes 4718600 | tf_op jit(solution)/shard_map/ppermute | solution.py:9
  33.2 57.9 %copy-start.1 = (bf16[32,24576]{1,0:T(8,128)(2,1)}, bf16[32,24576]{1,0:T(8,128)(2,1)S(1)}, u32[]{:S(2)}) copy-start(bf16[32,24576]{1,0:T(8,128)(2,1)S(1)} %collective-permute-done.1) | copy-start | bytes 4718596
  33.2 25.2 %collective-permute-start.3 = (bf16[32,24576]{1,0:T(8,128)(2,1)S(1)}, bf16[32,24576]{1,0:T(8,128)(2,1)S(1)}, u32[]{:S(2)}, u32[]{:S(2)}) collective-permute-start(bf16[32,24576]{1,0:T(8,128)(2,1)S(1)} %collective-permute-done.1), channel_id=1, source_target_pairs={{0,255},{1,0},{2,1},{3,2},{4,3},{5,4},{6,5},{7,6},{8,7},{9,8},{10,... | collective-permute-start | bytes 4718600 | tf_op jit(solution)/shard_map/ppermute | solution.py:9
  40.5 50.7 %copy-start.7 = (bf16[32,24576]{1,0:T(8,128)(2,1)}, bf16[32,24576]{1,0:T(8,128)(2,1)S(1)}, u32[]{:S(2)}) copy-start(bf16[32,24576]{1,0:T(8,128)(2,1)S(1)} %collective-permute-done) | copy-start | bytes 4718596
  40.5 25.3 %collective-permute-start.2 = (bf16[32,24576]{1,0:T(8,128)(2,1)S(1)}, bf16[32,24576]{1,0:T(8,128)(2,1)S(1)}, u32[]{:S(2)}, u32[]{:S(2)}) collective-permute-start(bf16[32,24576]{1,0:T(8,128)(2,1)S(1)} %collective-permute-done), channel_id=1, source_target_pairs={{0,1},{1,2},{2,3},{3,4},{4,5},{5,6},{6,7},{7,8},{8,9},{9,10},{10,1... | collective-permute-start | bytes 4718600 | tf_op jit(solution)/shard_map/ppermute | solution.py:9
  58.4 32.7 %copy-start.3 = (bf16[32,24576]{1,0:T(8,128)(2,1)}, bf16[32,24576]{1,0:T(8,128)(2,1)S(1)}, u32[]{:S(2)}) copy-start(bf16[32,24576]{1,0:T(8,128)(2,1)S(1)} %collective-permute-done.3) | copy-start | bytes 4718596
  58.4 25.3 %collective-permute-start.5 = (bf16[32,24576]{1,0:T(8,128)(2,1)S(1)}, bf16[32,24576]{1,0:T(8,128)(2,1)S(1)}, u32[]{:S(2)}, u32[]{:S(2)}) collective-permute-start(bf16[32,24576]{1,0:T(8,128)(2,1)S(1)} %collective-permute-done.3), channel_id=1, source_target_pairs={{0,255},{1,0},{2,1},{3,2},{4,3},{5,4},{6,5},{7,6},{8,7},{9,8},{10,... | collective-permute-start | bytes 4718600 | tf_op jit(solution)/shard_map/ppermute | solution.py:9
  65.7 25.4 %collective-permute-start.4 = (bf16[32,24576]{1,0:T(8,128)(2,1)S(1)}, bf16[32,24576]{1,0:T(8,128)(2,1)}, u32[]{:S(2)}, u32[]{:S(2)}) collective-permute-start(bf16[32,24576]{1,0:T(8,128)(2,1)S(1)} %collective-permute-done.2), channel_id=1, source_target_pairs={{0,1},{1,2},{2,3},{3,4},{4,5},{5,6},{6,7},{7,8},{8,9},{9,10},{10,1... | collective-permute-start | bytes 4718600 | tf_op jit(solution)/shard_map/ppermute | solution.py:9
  83.7 7.5 %copy-start.5 = (bf16[32,24576]{1,0:T(8,128)(2,1)}, bf16[32,24576]{1,0:T(8,128)(2,1)S(1)}, u32[]{:S(2)}) copy-start(bf16[32,24576]{1,0:T(8,128)(2,1)S(1)} %collective-permute-done.5) | copy-start | bytes 4718596
  83.7 25.3 %collective-permute-start.7 = (bf16[32,24576]{1,0:T(8,128)(2,1)S(1)}, bf16[32,24576]{1,0:T(8,128)(2,1)}, u32[]{:S(2)}, u32[]{:S(2)}) collective-permute-start(bf16[32,24576]{1,0:T(8,128)(2,1)S(1)} %collective-permute-done.5), channel_id=1, source_target_pairs={{0,255},{1,0},{2,1},{3,2},{4,3},{5,4},{6,5},{7,6},{8,7},{9,8},{10,... | collective-permute-start | bytes 4718600 | tf_op jit(solution)/shard_map/ppermute | solution.py:9
  91.1 26.6 %collective-permute-start.6 = (bf16[32,24576]{1,0:T(8,128)(2,1)}, bf16[32,24576]{1,0:T(8,128)(2,1)S(1)}, u32[]{:S(2)}, u32[]{:S(2)}) collective-permute-start(bf16[32,24576]{1,0:T(8,128)(2,1)} %collective-permute-done.4), channel_id=1, source_target_pairs={{0,1},{1,2},{2,3},{3,4},{4,5},{5,6},{6,7},{7,8},{8,9},{9,10},{10,1... | collective-permute-start | bytes 4718600 | tf_op jit(solution)/shard_map/ppermute | solution.py:9
  108.9 25.7 %collective-permute-start.9 = (bf16[32,24576]{1,0:T(8,128)(2,1)}, bf16[32,24576]{1,0:T(8,128)(2,1)}, u32[]{:S(2)}, u32[]{:S(2)}) collective-permute-start(bf16[32,24576]{1,0:T(8,128)(2,1)} %collective-permute-done.7), channel_id=1, source_target_pairs={{0,255},{1,0},{2,1},{3,2},{4,3},{5,4},{6,5},{7,6},{8,7},{9,8},{10,... | collective-permute-start | bytes 4718600 | tf_op jit(solution)/shard_map/ppermute | solution.py:9
  117.7 25.5 %collective-permute-start.8 = (bf16[32,24576]{1,0:T(8,128)(2,1)S(1)}, bf16[32,24576]{1,0:T(8,128)(2,1)}, u32[]{:S(2)}, u32[]{:S(2)}) collective-permute-start(bf16[32,24576]{1,0:T(8,128)(2,1)S(1)} %collective-permute-done.6), channel_id=1, source_target_pairs={{0,1},{1,2},{2,3},{3,4},{4,5},{5,6},{6,7},{7,8},{8,9},{9,10},{10,1... | collective-permute-start | bytes 4718600 | tf_op jit(solution)/shard_map/ppermute | solution.py:9
  118.1 2.1 copy-start.8
  120.2 1.4 copy-start.2
  121.6 20.3 %copy-start.4 = (bf16[32,24576]{1,0:T(8,128)(2,1)S(1)}, bf16[32,24576]{1,0:T(8,128)(2,1)}, u32[]{:S(2)}) copy-start(bf16[32,24576]{1,0:T(8,128)(2,1)} %copy-done.3) | copy-start | bytes 4718596
  134.6 25.6 %collective-permute-start.11 = (bf16[32,24576]{1,0:T(8,128)(2,1)}, bf16[32,24576]{1,0:T(8,128)(2,1)S(1)}, u32[]{:S(2)}, u32[]{:S(2)}) collective-permute-start(bf16[32,24576]{1,0:T(8,128)(2,1)} %collective-permute-done.9), channel_id=1, source_target_pairs={{0,255},{1,0},{2,1},{3,2},{4,3},{5,4},{6,5},{7,6},{8,7},{9,8},{10,... | collective-permute-start | bytes 4718600 | tf_op jit(solution)/shard_map/ppermute | solution.py:9
  142.6 1.4 copy-start.6
  143.2 26.2 %collective-permute-start.10 = (bf16[32,24576]{1,0:T(8,128)(2,1)}, bf16[32,24576]{1,0:T(8,128)(2,1)S(1)}, u32[]{:S(2)}, u32[]{:S(2)}) collective-permute-start(bf16[32,24576]{1,0:T(8,128)(2,1)} %collective-permute-done.8), channel_id=1, source_target_pairs={{0,1},{1,2},{2,3},{3,4},{4,5},{5,6},{6,7},{7,8},{8,9},{9,10},{10,1... | collective-permute-start | bytes 4718600 | tf_op jit(solution)/shard_map/ppermute | solution.py:9
  160.2 25.2 %collective-permute-start.13 = (bf16[32,24576]{1,0:T(8,128)(2,1)S(1)}, bf16[32,24576]{1,0:T(8,128)(2,1)S(1)}, u32[]{:S(2)}, u32[]{:S(2)}) collective-permute-start(bf16[32,24576]{1,0:T(8,128)(2,1)S(1)} %collective-permute-done.11), channel_id=1, source_target_pairs={{0,255},{1,0},{2,1},{3,2},{4,3},{5,4},{6,5},{7,6},{8,7},{9,8},{10,... | collective-permute-start | bytes 4718600 | tf_op jit(solution)/shard_map/ppermute | solution.py:9
  169.4 25.3 %collective-permute-start.12 = (bf16[32,24576]{1,0:T(8,128)(2,1)S(1)}, bf16[32,24576]{1,0:T(8,128)(2,1)S(1)}, u32[]{:S(2)}, u32[]{:S(2)}) collective-permute-start(bf16[32,24576]{1,0:T(8,128)(2,1)S(1)} %collective-permute-done.10), channel_id=1, source_target_pairs={{0,1},{1,2},{2,3},{3,4},{4,5},{5,6},{6,7},{7,8},{8,9},{9,10},{10,1... | collective-permute-start | bytes 4718600 | tf_op jit(solution)/shard_map/ppermute | solution.py:9
  185.4 25.3 %collective-permute-start.15 = (bf16[32,24576]{1,0:T(8,128)(2,1)S(1)}, bf16[32,24576]{1,0:T(8,128)(2,1)S(1)}, u32[]{:S(2)}, u32[]{:S(2)}) collective-permute-start(bf16[32,24576]{1,0:T(8,128)(2,1)S(1)} %collective-permute-done.13), channel_id=1, source_target_pairs={{0,255},{1,0},{2,1},{3,2},{4,3},{5,4},{6,5},{7,6},{8,7},{9,8},{10,... | collective-permute-start | bytes 4718600 | tf_op jit(solution)/shard_map/ppermute | solution.py:9
  194.8 25.3 %collective-permute-start.14 = (bf16[32,24576]{1,0:T(8,128)(2,1)S(1)}, bf16[32,24576]{1,0:T(8,128)(2,1)S(1)}, u32[]{:S(2)}, u32[]{:S(2)}) collective-permute-start(bf16[32,24576]{1,0:T(8,128)(2,1)S(1)} %collective-permute-done.12), channel_id=1, source_target_pairs={{0,1},{1,2},{2,3},{3,4},{4,5},{5,6},{6,7},{7,8},{8,9},{9,10},{10,1... | collective-permute-start | bytes 4718600 | tf_op jit(solution)/shard_map/ppermute | solution.py:9
  223.9 8.1 %copy-start.9 = (f32[32,3,2048]{2,0,1:T(8,128)S(1)}, f32[32,3,2048]{2,0,1:T(8,128)}, u32[]{:S(2)}) copy-start(f32[32,3,2048]{2,0,1:T(8,128)} %param.11) | copy-start | bytes 2359300
  232.0 0.7 copy-start.10
  232.5 0.9 copy-start
where the time goes:
time: 236 us
  waiting for transfers between devices  134 us (57%)
  starting transfers between devices  59.7 us (25%)
  matrix products  25.8 us (11%)
  local copies, waits for them, and re-layouts  13.4 us (6%)
    ppermute x16, waiting for transfers between devices, from_behind(): lax.ppermute(value, axis, [(i, (i + by) % count) for i in range(count)])  134 us
    ppermute x16, starting transfers between devices, from_behind(): lax.ppermute(value, axis, [(i, (i + by) % count) for i in range(count)])  59.7 us
    dot_general x1, matrix products, body(): lax.dot_general(spanned, wall_filter, (((3,), (1,)), ((), ())), preferred...  8.12 us
    dot_general x8, matrix products, body(): jnp.dot(tap_block(matrix, rows, -distance), below, preferred_element_type...  7.93 us
    dot_general x8, matrix products, body(): jnp.dot(tap_block(matrix, rows, distance), above, preferred_element_type=...  7.69 us
    unnamed x32, local copies, waits for them, and re-layouts  6.64 us
  transfers between devices with their start and end apart: 16, of which 12 were waited for; matrix products, arithmetic and copies ran while one was open for 8% of the time, Pallas kernels for 0%

commit v1 on v0

v1 whole, which is shorter than its diff:
```python
import jax
import jax.numpy as jnp
from jax import lax
from jax.experimental import pallas as pl
from jax.experimental.pallas import tpu as pltpu
from jax.sharding import PartitionSpec as P

MESH = pl.DeviceIdType.MESH
GROUP = 16
ROWS = 32
LANES = 128
HALF = 256
PEERS = [(0, 1)] + [(sign * far, other) for far in (1, 2, 3) for sign in (1, -1) for other in (0, 1)] + [(4, 0), (4, 1)]


def slot_of(far, other):
    return (far % 8) * 2 + other


def kernel(
    x, wall, prev, weights, scale, mean, diag, off,
    velocity, final,
    held, spread, columns, made, spanned, wide, turned, band, state, carried, sums, moving, mixed, shown,
    vweights, vscale, vmean, vdiag, voff,
    in_send, in_recv, halo_send, halo_recv, out_send, out_recv, load_sem, own_sem, store_sem,
):
    devices = lax.axis_size("span")
    me = lax.axis_index("span")
    base = (me // GROUP) * GROUP
    pos = lax.rem(me, GROUP)
    chip = pos // 2
    core = lax.rem(pos, 2)

    def place(far, other):
        return lax.rem(chip + far + 8, 8) * 2 + lax.rem(core + other, 2)

    before = lax.rem(me + devices - GROUP, devices)
    after = lax.rem(me + GROUP, devices)

    loads = []
    for index, (source, target) in enumerate(
        ((weights, vweights), (scale, vscale), (mean, vmean), (diag, vdiag), (off, voff), (prev, state), (wall, wide))
    ):
        loads.append(pltpu.make_async_copy(source, target, load_sem.at[index]))
        loads[-1].start()
    own = []
    for c in range(3):
        own.append(
            pltpu.make_async_copy(
                x.at[:, c, :, pl.ds(pl.multiple_of(pos * LANES, LANES), LANES)], held.at[c, 8 + pos], own_sem.at[c]
            )
        )
        own[-1].start()

    barrier = pltpu.get_barrier_semaphore()
    for far, other in PEERS:
        pl.semaphore_signal(barrier, inc=1, device_id=(base + place(far, other),), device_id_type=MESH)
    for device in (before, after):
        pl.semaphore_signal(barrier, inc=1, device_id=(device,), device_id_type=MESH)
    pl.semaphore_wait(barrier, len(PEERS) + 2)

    arriving = []
    for c in range(3):
        arriving.append([])
        for far, other in PEERS:
            there = place(far, other)
            slot = slot_of(far, other)
            arriving[c].append(
                pltpu.make_async_remote_copy(
                    src_ref=x.at[:, c, :, pl.ds(pl.multiple_of(there * LANES, LANES), LANES)],
                    dst_ref=held.at[c, 8 + pos],
                    send_sem=in_send.at[c, slot],
                    recv_sem=in_recv.at[c, slot],
                    device_id=(base + there,),
                    device_id_type=MESH,
                )
            )
            arriving[c][-1].start()

    loads[0].wait()
    taps = vweights[...]
    taps = (taps / jnp.sqrt(jnp.sum(taps * taps))).astype(jnp.bfloat16).astype(jnp.float32)
    padded = jnp.concatenate([taps, jnp.zeros((1, 1024 - taps.shape[1]), jnp.float32)], axis=1)
    rolled = pltpu.roll(jnp.broadcast_to(padded, (HALF, 1024)), 0, 1, stride=1, stride_axis=0)
    band[...] = rolled[:, : 3 * HALF].astype(jnp.bfloat16)

    loads[6].wait()
    one = (
        lax.broadcasted_iota(jnp.int32, (256, 256), 0) == lax.broadcasted_iota(jnp.int32, (256, 256), 1)
    ).astype(jnp.bfloat16)

    def turn(step, carry):
        row = pl.multiple_of(step * 256, 256)
        for block in range(8):
            piece = wide[pl.ds(row, 256), block * 256 : (block + 1) * 256]
            turned[block * 256 : (block + 1) * 256, pl.ds(row, 256)] = lax.dot_general(
                one, piece, (((1,), (1,)), ((), ())), preferred_element_type=jnp.float32
            ).astype(jnp.bfloat16)
        return carry

    lax.fori_loop(0, 8, turn, 0)

    for index in range(1, 6):
        loads[index].wait()

    flat = held.reshape(3 * 32 * ROWS * 4, LANES)

    def unpack(c, slot):
        first = pl.multiple_of((c * 32 + slot) * LANES, LANES)
        row = pl.multiple_of(slot * LANES, LANES)
        spread[pl.ds(row, LANES), :] = flat[pl.ds(first, LANES), :].astype(jnp.float32)
        for t in range(4):
            columns[pl.ds(pl.multiple_of(slot * ROWS, ROWS), ROWS), t * LANES : (t + 1) * LANES] = spread[
                pl.ds(row + t, ROWS, stride=4), :
            ].astype(jnp.bfloat16)

    halos = []
    leaving = []
    for c in range(3):
        own[c].wait()
        for copy in arriving[c]:
            copy.wait_recv()
        halos.append([])
        for index, (source, target, device) in enumerate(((8, 24, before), (16, 0, after))):
            halos[c].append(
                pltpu.make_async_remote_copy(
                    src_ref=held.at[c, pl.ds(source, 8)],
                    dst_ref=held.at[c, pl.ds(target, 8)],
                    send_sem=halo_send.at[c, index],
                    recv_sem=halo_recv.at[c, index],
                    device_id=(device,),
                    device_id_type=MESH,
                )
            )
            halos[c][-1].start()

        def middle(step, carry):
            for part in range(4):
                unpack(c, 8 + step * 4 + part)
            return carry

        lax.fori_loop(0, 4, middle, 0)
        for copy in halos[c]:
            copy.wait_recv()

        def outer(step, carry):
            for part in range(4):
                unpack(c, step * 4 + part)
                unpack(c, 24 + step * 4 + part)
            return carry

        lax.fori_loop(0, 2, outer, 0)
        for half in range(2):
            block = jnp.dot(
                band[...], columns[half * HALF : half * HALF + 3 * HALF, :], preferred_element_type=jnp.float32
            ).astype(jnp.bfloat16)
            for t in range(4):
                made[c, t, half * HALF : (half + 1) * HALF, :] = block[:, t * LANES : (t + 1) * LANES]
        spanned[c, :, :, pl.ds(pl.multiple_of(pos * LANES, LANES), LANES)] = made[
            c, :, pl.ds(pl.multiple_of(pos * ROWS, ROWS), ROWS), :
        ]
        leaving.append([])
        for far, other in PEERS:
            there = place(far, other)
            slot = slot_of(far, other)
            leaving[c].append(
                pltpu.make_async_remote_copy(
                    src_ref=made.at[c, :, pl.ds(pl.multiple_of(there * ROWS, ROWS), ROWS), :],
                    dst_ref=spanned.at[c, :, :, pl.ds(pl.multiple_of(pos * LANES, LANES), LANES)],
                    send_sem=out_send.at[c, slot],
                    recv_sem=out_recv.at[c, slot],
                    device_id=(base + there,),
                    device_id_type=MESH,
                )
            )
            leaving[c][-1].start()

    stores = []
    for c in range(3):
        for index, far in enumerate((0, 1, -1, 2, -2, 3, -3, 4)):
            for copy, peer in zip(leaving[c], PEERS):
                if peer[0] == far:
                    copy.wait_recv()
            origin = pl.multiple_of(lax.rem(chip - far + 8, 8) * 256, 256)
            piece = spanned[c, :, :, pl.ds(origin, 256)].reshape(4 * ROWS, 256)
            term = jnp.dot(piece, turned[pl.ds(origin, 256), :], preferred_element_type=jnp.float32)
            if index == 0:
                sums[...] = term
            else:
                sums[...] += term
        for block in range(8):
            cols = slice(block * 256, (block + 1) * 256)
            time = vscale[c : c + 1, cols]
            decay = jnp.exp(-jnp.pi / (2.0 * time))
            inject = jnp.sqrt(1.0 - jnp.exp(-jnp.pi / time))
            value = state[c, :, cols]
            for t in range(4):
                value = decay * value + inject * sums[t * ROWS : (t + 1) * ROWS, cols]
                if c == 0:
                    carried[0, t, :, cols] = value
                    out = vmean[:, cols] + vdiag[0:1, cols] * value
                elif c == 1:
                    along = carried[0, t, :, cols]
                    out = voff[0:1, cols] * along + vdiag[1:2, cols] * value
                    carried[0, t, :, cols] = voff[1:2, cols] * along + voff[2:3, cols] * value
                else:
                    out = carried[0, t, :, cols] + vdiag[2:3, cols] * value
                for side in range(2):
                    mixed[2 * block + side, pl.ds(t, ROWS, stride=4), :] = out[:, side * LANES : (side + 1) * LANES]
            shown[c, :, cols] = value
            for tile in (2 * block, 2 * block + 1):
                moving[c, :, :, tile * LANES : (tile + 1) * LANES] = (
                    mixed[tile].reshape(ROWS, 4, LANES).astype(jnp.bfloat16)
                )
        stores.append(pltpu.make_async_copy(shown.at[c], final.at[c], store_sem.at[0, c]))
        stores[-1].start()
        stores.append(pltpu.make_async_copy(moving.at[c], velocity.at[:, c], store_sem.at[1, c]))
        stores[-1].start()

    for c in range(3):
        for copy in arriving[c] + halos[c] + leaving[c]:
            copy.wait_send()
    for copy in stores:
        copy.wait()


def body(random_slabs, span_weights, wall_filter, prev_state, time_scale, mean_velocity, lund_diag, lund_off):
    rows, planes, parts, width = random_slabs.shape
    any_spec = pl.BlockSpec(memory_space=pl.ANY)
    bf16, f32 = jnp.bfloat16, jnp.float32
    velocity, state = pl.pallas_call(
        kernel,
        out_shape=(
            jax.ShapeDtypeStruct((rows, parts, planes, width), bf16),
            jax.ShapeDtypeStruct((parts, rows, width), f32),
        ),
        in_specs=[any_spec] * 8,
        out_specs=(any_spec, any_spec),
        scratch_shapes=[
            pltpu.VMEM((3, 32, ROWS, 4, LANES), bf16),
            pltpu.VMEM((4096, LANES), f32),
            pltpu.VMEM((1024, 4 * LANES), bf16),
            pltpu.VMEM((3, 4, 512, LANES), bf16),
            pltpu.VMEM((3, 4, ROWS, width), bf16),
            pltpu.VMEM((width, width), bf16),
            pltpu.VMEM((width, width), bf16),
            pltpu.VMEM((HALF, 3 * HALF), bf16),
            pltpu.VMEM((3, ROWS, width), f32),
            pltpu.VMEM((1, 4, ROWS, width), f32),
            pltpu.VMEM((4 * ROWS, width), f32),
            pltpu.VMEM((3, ROWS, 4, width), bf16),
            pltpu.VMEM((width // LANES, 4 * ROWS, LANES), f32),
            pltpu.VMEM((3, ROWS, width), f32),
            pltpu.VMEM((1, 2 * HALF + 1), f32),
            pltpu.VMEM((3, width), f32),
            pltpu.VMEM((1, width), f32),
            pltpu.VMEM((3, width), f32),
            pltpu.VMEM((3, width), f32),
            pltpu.SemaphoreType.DMA((3, 16)),
            pltpu.SemaphoreType.DMA((3, 16)),
            pltpu.SemaphoreType.DMA((3, 2)),
            pltpu.SemaphoreType.DMA((3, 2)),
            pltpu.SemaphoreType.DMA((3, 16)),
            pltpu.SemaphoreType.DMA((3, 16)),
            pltpu.SemaphoreType.DMA((7,)),
            pltpu.SemaphoreType.DMA((3,)),
            pltpu.SemaphoreType.DMA((2, 3)),
        ],
        compiler_params=pltpu.CompilerParams(collective_id=0, has_side_effects=True, vmem_limit_bytes=60 * 2**20),
        name="inflow",
    )(
        random_slabs.transpose(0, 2, 1, 3),
        wall_filter,
        prev_state.transpose(1, 0, 2),
        span_weights.reshape(1, -1),
        time_scale,
        mean_velocity.reshape(1, -1),
        lund_diag,
        lund_off,
    )
    return velocity.transpose(0, 2, 1, 3), state.transpose(1, 0, 2)


def solution(mesh):
    placed = (P("span", None, None, None), P(), P(), P("span", None, None), P(), P(), P(), P())
    return jax.shard_map(
        body,
        mesh=mesh,
        in_specs=placed,
        out_specs=(P("span", None, None, None), P("span", None, None)),
        check_vma=False,
    )
```

time: 236 us -> 91.2 us (0.39)
  the two profiles are of different devices: /device:TPU:0 before, /device:TPU:1 now
where the time goes in v1:
time: 91.2 us; the launch traced here: 91 us
  Pallas kernels  84.8 us (93%)
  local copies, waits for them, and re-layouts  5.56 us (6%)
    pallas_call x1, Pallas kernels, body(): pl.pallas_call(kernel, out_shape=(jax.ShapeDtypeStruct((rows, parts, plan...  84.8 us
    unnamed x4, local copies, waits for them, and re-layouts  4.3 us

profile of v1, /device:TPU:1, one launch (start us, length us, event | category | flops | bytes accessed | tf_op | source)
XLA Modules:
  0.0 91.0 jit_solution(5659459439258910626)
XLA Ops:
  0.6 1.3 %reshape.10.weights = f32[1,513]{1,0:T(1,128)} reshape(f32[513]{0:T(1024)} %param.9) | data formatting | bytes 4104 | tf_op jit(solution)/shard_map/reshape | solution.py:275
  1.9 84.8 %inflow.1 = (bf16[32,3,4,2048]{3,2,1,0:T(4,128)(2,1)}, f32[3,32,2048]{2,1,0:T(8,128)}) custom-call(bf16[32,3,4,2048]{3,2,1,0:T(4,128)(2,1)} %bitcast.6, bf16[2048,2048]{1,0:T(8,128)(2,1)} %wall.1, f32[3,32,2048]{2,1,0:T(8,128)} %bitcast.8, f32[1,513]{1,0:T(1,128)} %reshape.10.weights, f32[3,2048]{1,0:T(4,128)} %scale.1, f32[1,2048]{1,0:T(1,128)} %bitcast.9, ...), custom_call_target="tpu_custom_call" | custom-call | tf_op jit(solution)/shard_map/inflow/pallas_call | solution.py:231
  86.7 0.0 copy-start
  86.7 3.4 %copy.12 = bf16[32,4,3,2048]{3,1,2,0:T(4,128)(2,1)} copy(bf16[32,4,3,2048]{3,1,2,0:T(4,128)(2,1)} %bitcast.5) | data formatting | bytes 3145728
  90.2 0.0 copy-done
  90.2 0.9 copy.13
Async XLA Ops:
  86.7 3.4 %copy-start = (f32[3,32,2048]{2,1,0:T(8,128)S(1)}, f32[3,32,2048]{2,1,0:T(8,128)}, u32[]{:S(2)}) copy-start(f32[3,32,2048]{2,1,0:T(8,128)} %get-tuple-element.5) | copy-start | bytes 2359300

commit v2 on v1

--- a/solution.py
+++ b/solution.py
@@ -19,10 +19,10 @@
 
 def kernel(
     x, wall, prev, weights, scale, mean, diag, off,
-    velocity, final,
-    held, spread, columns, made, spanned, wide, turned, band, state, carried, sums, moving, mixed, shown,
+    moving, shown,
+    held, spread, columns, made, spanned, wide, turned, band, state, carried, sums, mixed,
     vweights, vscale, vmean, vdiag, voff,
-    in_send, in_recv, halo_send, halo_recv, out_send, out_recv, load_sem, own_sem, store_sem,
+    in_send, in_recv, halo_send, halo_recv, out_send, out_recv, load_sem, own_sem,
 ):
     devices = lax.axis_size("span")
     me = lax.axis_index("span")
@@ -78,7 +78,7 @@
             arriving[c][-1].start()
 
     loads[0].wait()
-    taps = vweights[...]
+    taps = vweights[...].reshape(1, 2 * HALF + 1)
     taps = (taps / jnp.sqrt(jnp.sum(taps * taps))).astype(jnp.bfloat16).astype(jnp.float32)
     padded = jnp.concatenate([taps, jnp.zeros((1, 1024 - taps.shape[1]), jnp.float32)], axis=1)
     rolled = pltpu.roll(jnp.broadcast_to(padded, (HALF, 1024)), 0, 1, stride=1, stride_axis=0)
@@ -160,7 +160,7 @@
             c, :, pl.ds(pl.multiple_of(pos * ROWS, ROWS), ROWS), :
         ]
         leaving.append([])
-        for far, other in PEERS:
+        for far, other in (PEERS if c < 2 else PEERS[::-1]):
             there = place(far, other)
             slot = slot_of(far, other)
             leaving[c].append(
@@ -175,10 +175,9 @@
             )
             leaving[c][-1].start()
 
-    stores = []
-    for c in range(3):
-        for index, far in enumerate((0, 1, -1, 2, -2, 3, -3, 4)):
-            for copy, peer in zip(leaving[c], PEERS):
+    for c in range(3):
+        for index, far in enumerate((0, 1, -1, 2, -2, 3, -3, 4) if c < 2 else (4, -3, 3, -2, 2, -1, 1, 0)):
+            for copy, peer in zip(leaving[c], PEERS if c < 2 else PEERS[::-1]):
                 if peer[0] == far:
                     copy.wait_recv()
             origin = pl.multiple_of(lax.rem(chip - far + 8, 8) * 256, 256)
@@ -212,15 +211,20 @@
                 moving[c, :, :, tile * LANES : (tile + 1) * LANES] = (
                     mixed[tile].reshape(ROWS, 4, LANES).astype(jnp.bfloat16)
                 )
-        stores.append(pltpu.make_async_copy(shown.at[c], final.at[c], store_sem.at[0, c]))
-        stores[-1].start()
-        stores.append(pltpu.make_async_copy(moving.at[c], velocity.at[:, c], store_sem.at[1, c]))
-        stores[-1].start()
 
     for c in range(3):
         for copy in arriving[c] + halos[c] + leaving[c]:
             copy.wait_send()
-    for copy in stores:
+
+
+def finish(moving, shown, velocity, final, sems):
+    copies = []
+    for c in range(3):
+        copies.append(pltpu.make_async_copy(moving.at[c], velocity.at[:, c], sems.at[0, c]))
+        copies.append(pltpu.make_async_copy(shown.at[c], final.at[c], sems.at[1, c]))
+    for copy in copies:
+        copy.start()
+    for copy in copies:
         copy.wait()
 
 
@@ -228,14 +232,14 @@
     rows, planes, parts, width = random_slabs.shape
     any_spec = pl.BlockSpec(memory_space=pl.ANY)
     bf16, f32 = jnp.bfloat16, jnp.float32
-    velocity, state = pl.pallas_call(
+    moving, shown = pl.pallas_call(
         kernel,
         out_shape=(
-            jax.ShapeDtypeStruct((rows, parts, planes, width), bf16),
-            jax.ShapeDtypeStruct((parts, rows, width), f32),
+            pltpu.VMEM((parts, rows, planes, width), bf16),
+            pltpu.VMEM((parts, rows, width), f32),
         ),
         in_specs=[any_spec] * 8,
-        out_specs=(any_spec, any_spec),
+        out_specs=(pl.BlockSpec(memory_space=pltpu.VMEM),) * 2,
         scratch_shapes=[
             pltpu.VMEM((3, 32, ROWS, 4, LANES), bf16),
             pltpu.VMEM((4096, LANES), f32),
@@ -248,10 +252,8 @@
             pltpu.VMEM((3, ROWS, width), f32),
             pltpu.VMEM((1, 4, ROWS, width), f32),
             pltpu.VMEM((4 * ROWS, width), f32),
-            pltpu.VMEM((3, ROWS, 4, width), bf16),
             pltpu.VMEM((width // LANES, 4 * ROWS, LANES), f32),
-            pltpu.VMEM((3, ROWS, width), f32),
-            pltpu.VMEM((1, 2 * HALF + 1), f32),
+            pltpu.VMEM((2 * HALF + 1,), f32),
             pltpu.VMEM((3, width), f32),
             pltpu.VMEM((1, width), f32),
             pltpu.VMEM((3, width), f32),
@@ -264,7 +266,6 @@
             pltpu.SemaphoreType.DMA((3, 16)),
             pltpu.SemaphoreType.DMA((7,)),
             pltpu.SemaphoreType.DMA((3,)),
-            pltpu.SemaphoreType.DMA((2, 3)),
         ],
         compiler_params=pltpu.CompilerParams(collective_id=0, has_side_effects=True, vmem_limit_bytes=60 * 2**20),
         name="inflow",
@@ -272,12 +273,24 @@
         random_slabs.transpose(0, 2, 1, 3),
         wall_filter,
         prev_state.transpose(1, 0, 2),
-        span_weights.reshape(1, -1),
+        span_weights,
         time_scale,
         mean_velocity.reshape(1, -1),
         lund_diag,
         lund_off,
     )
+    velocity, state = pl.pallas_call(
+        finish,
+        out_shape=(
+            jax.ShapeDtypeStruct((rows, parts, planes, width), bf16),
+            jax.ShapeDtypeStruct((parts, rows, width), f32),
+        ),
+        in_specs=[pl.BlockSpec(memory_space=pltpu.VMEM)] * 2,
+        out_specs=(any_spec, any_spec),
+        scratch_shapes=[pltpu.SemaphoreType.DMA((2, 3))],
+        compiler_params=pltpu.CompilerParams(vmem_limit_bytes=8 * 2**20),
+        name="finish",
+    )(pltpu.with_memory_space_constraint(moving, pltpu.VMEM), pltpu.with_memory_space_constraint(shown, pltpu.VMEM))
     return velocity.transpose(0, 2, 1, 3), state.transpose(1, 0, 2)
 
 

time: 91.2 us -> 84.9 us (0.931)
  local copies, waits for them, and re-layouts: 5.56 us -> 0 us
    unnamed x4 -> x0, local copies, waits for them, and re-layouts: 4.3 us -> none
    reshape x1 -> x0, local copies, waits for them, and re-layouts: 1.27 us -> none  [body(): span_weights.reshape(1, -1)]
    pallas_call x1 -> x2, Pallas kernels: 84.8 us -> 84.2 us  [the longest x1 82.7 us: body(): pl.pallas_call(kernel, out_shape=(pltpu.VMEM((parts, rows, planes, width)...]
where the time goes in v2:
time: 84.9 us; the launch traced here: 84.8 us
  Pallas kernels  84.2 us (99%)
    pallas_call x1, Pallas kernels, body(): pl.pallas_call(kernel, out_shape=(pltpu.VMEM((parts, rows, planes, width)...  82.7 us

profile of v2, /device:TPU:1, one launch (start us, length us, event | category | flops | bytes accessed | tf_op | source)
XLA Modules:
  0.0 84.8 jit_solution(17540546694677432530)
XLA Ops:
  0.6 82.7 %inflow.1 = (bf16[3,32,4,2048]{3,2,1,0:T(4,128)(2,1)S(1)}, f32[3,32,2048]{2,1,0:T(8,128)S(1)}) custom-call(bf16[32,3,4,2048]{3,2,1,0:T(4,128)(2,1)} %bitcast.5, bf16[2048,2048]{1,0:T(8,128)(2,1)} %wall.1, f32[3,32,2048]{2,1,0:T(8,128)} %bitcast.6, f32[513]{0:T(1024)} %weights.1, f32[3,2048]{1,0:T(4,128)} %scale.1, f32[1,2048]{1,0:T(1,128)} %bitcast.7, ...), custom_call_target="tpu_custom_call" | custom-call | tf_op jit(solution)/shard_map/inflow/pallas_call | solution.py:235
  83.4 1.4 %finish.1 = (bf16[32,3,4,2048]{3,2,1,0:T(4,128)(2,1)}, f32[3,32,2048]{2,1,0:T(8,128)}) custom-call(bf16[3,32,4,2048]{3,2,1,0:T(4,128)(2,1)S(1)} %get-tuple-element.6.moving, f32[3,32,2048]{2,1,0:T(8,128)S(1)} %get-tuple-element.7.shown), custom_call_target="tpu_custom_call" | custom-call | tf_op jit(solution)/shard_map/finish/pallas_call | solution.py:282

commit v3 on v2

--- a/solution.py
+++ b/solution.py
@@ -13,8 +13,12 @@
 PEERS = [(0, 1)] + [(sign * far, other) for far in (1, 2, 3) for sign in (1, -1) for other in (0, 1)] + [(4, 0), (4, 1)]
 
 
-def slot_of(far, other):
-    return (far % 8) * 2 + other
+NEAR = PEERS[:5]
+SCOUT = 8
+
+
+def wait_for(view, sem):
+    pltpu.make_async_copy(view, view, sem).wait()
 
 
 def kernel(
@@ -22,7 +26,7 @@
     moving, shown,
     held, spread, columns, made, spanned, wide, turned, band, state, carried, sums, mixed,
     vweights, vscale, vmean, vdiag, voff,
-    in_send, in_recv, halo_send, halo_recv, out_send, out_recv, load_sem, own_sem,
+    in_send, in_recv, halo_send, halo_recv, out_send, out_recv, last_recv, load_sem, chain, scouts, release,
 ):
     devices = lax.axis_size("span")
     me = lax.axis_index("span")
@@ -37,45 +41,70 @@
     before = lax.rem(me + devices - GROUP, devices)
     after = lax.rem(me + GROUP, devices)
 
+    scout = pos == SCOUT
+    barrier = pltpu.get_barrier_semaphore()
+    for far, other in NEAR:
+        pl.semaphore_signal(barrier, inc=1, device_id=(base + place(far, other),), device_id_type=MESH)
+
+    @pl.when(scout)
+    def _():
+        for device in (before, after):
+            pl.semaphore_signal(barrier, inc=1, device_id=(device,), device_id_type=MESH)
+
     loads = []
     for index, (source, target) in enumerate(
         ((weights, vweights), (scale, vscale), (mean, vmean), (diag, vdiag), (off, voff), (prev, state), (wall, wide))
     ):
         loads.append(pltpu.make_async_copy(source, target, load_sem.at[index]))
         loads[-1].start()
-    own = []
     for c in range(3):
-        own.append(
-            pltpu.make_async_copy(
-                x.at[:, c, :, pl.ds(pl.multiple_of(pos * LANES, LANES), LANES)], held.at[c, 8 + pos], own_sem.at[c]
-            )
-        )
-        own[-1].start()
-
-    barrier = pltpu.get_barrier_semaphore()
-    for far, other in PEERS:
-        pl.semaphore_signal(barrier, inc=1, device_id=(base + place(far, other),), device_id_type=MESH)
-    for device in (before, after):
-        pl.semaphore_signal(barrier, inc=1, device_id=(device,), device_id_type=MESH)
-    pl.semaphore_wait(barrier, len(PEERS) + 2)
-
-    arriving = []
-    for c in range(3):
-        arriving.append([])
+        pltpu.make_async_copy(
+            x.at[:, c, :, pl.ds(pl.multiple_of(pos * LANES, LANES), LANES)], held.at[c, 8 + pos], in_recv.at[c]
+        ).start()
+
+    def send_in(c, far, other):
+        there = place(far, other)
+        pltpu.make_async_remote_copy(
+            src_ref=x.at[:, c, :, pl.ds(pl.multiple_of(there * LANES, LANES), LANES)],
+            dst_ref=held.at[c, 8 + pos],
+            send_sem=in_send,
+            recv_sem=in_recv.at[c],
+            device_id=(base + there,),
+            device_id_type=MESH,
+        ).start()
+
+    @pl.when(scout)
+    def _():
+        pl.semaphore_wait(barrier, len(NEAR) + 2)
+
+    @pl.when(jnp.logical_not(scout))
+    def _():
+        pl.semaphore_wait(barrier, len(NEAR))
+
+    for far, other in NEAR:
+        send_in(0, far, other)
+    for stage, reach in enumerate(((2, -2), (3, -3), (4,))):
+
+        @pl.when(core == 1)
+        def _():
+            for sign in (1, -1):
+                for other in (0, 1):
+                    pl.semaphore_signal(
+                        chain.at[stage], inc=1, device_id=(base + place(sign, other),), device_id_type=MESH
+                    )
+
+        pl.semaphore_wait(chain.at[stage], 2)
+        for far in reach:
+            for other in (0, 1):
+                send_in(0, far, other)
+    for c in (1, 2):
         for far, other in PEERS:
-            there = place(far, other)
-            slot = slot_of(far, other)
-            arriving[c].append(
-                pltpu.make_async_remote_copy(
-                    src_ref=x.at[:, c, :, pl.ds(pl.multiple_of(there * LANES, LANES), LANES)],
-                    dst_ref=held.at[c, 8 + pos],
-                    send_sem=in_send.at[c, slot],
-                    recv_sem=in_recv.at[c, slot],
-                    device_id=(base + there,),
-                    device_id_type=MESH,
-                )
-            )
-            arriving[c][-1].start()
+            send_in(c, far, other)
+
+    @pl.when(scout)
+    def _():
+        for device in (before, after):
+            pl.semaphore_signal(scouts, inc=1, device_id=(device,), device_id_type=MESH)
 
     loads[0].wait()
     taps = vweights[...].reshape(1, 2 * HALF + 1)
@@ -103,6 +132,16 @@
     for index in range(1, 6):
         loads[index].wait()
 
+    @pl.when(scout)
+    def _():
+        pl.semaphore_wait(scouts, 2)
+        for far, other in PEERS:
+            pl.semaphore_signal(release, inc=1, device_id=(base + place(far, other),), device_id_type=MESH)
+
+    @pl.when(jnp.logical_not(scout))
+    def _():
+        pl.semaphore_wait(release, 1)
+
     flat = held.reshape(3 * 32 * ROWS * 4, LANES)
 
     def unpack(c, slot):
@@ -114,25 +153,17 @@
                 pl.ds(row + t, ROWS, stride=4), :
             ].astype(jnp.bfloat16)
 
-    halos = []
-    leaving = []
     for c in range(3):
-        own[c].wait()
-        for copy in arriving[c]:
-            copy.wait_recv()
-        halos.append([])
-        for index, (source, target, device) in enumerate(((8, 24, before), (16, 0, after))):
-            halos[c].append(
-                pltpu.make_async_remote_copy(
-                    src_ref=held.at[c, pl.ds(source, 8)],
-                    dst_ref=held.at[c, pl.ds(target, 8)],
-                    send_sem=halo_send.at[c, index],
-                    recv_sem=halo_recv.at[c, index],
-                    device_id=(device,),
-                    device_id_type=MESH,
-                )
-            )
-            halos[c][-1].start()
+        wait_for(held.at[c, pl.ds(8, GROUP)], in_recv.at[c])
+        for source, target, device in ((8, 24, before), (16, 0, after)):
+            pltpu.make_async_remote_copy(
+                src_ref=held.at[c, pl.ds(source, 8)],
+                dst_ref=held.at[c, pl.ds(target, 8)],
+                send_sem=halo_send,
+                recv_sem=halo_recv.at[c],
+                device_id=(device,),
+                device_id_type=MESH,
+            ).start()
 
         def middle(step, carry):
             for part in range(4):
@@ -140,8 +171,7 @@
             return carry
 
         lax.fori_loop(0, 4, middle, 0)
-        for copy in halos[c]:
-            copy.wait_recv()
+        wait_for(held.at[c, pl.ds(8, GROUP)], halo_recv.at[c])
 
         def outer(step, carry):
             for part in range(4):
@@ -159,27 +189,23 @@
         spanned[c, :, :, pl.ds(pl.multiple_of(pos * LANES, LANES), LANES)] = made[
             c, :, pl.ds(pl.multiple_of(pos * ROWS, ROWS), ROWS), :
         ]
-        leaving.append([])
-        for far, other in (PEERS if c < 2 else PEERS[::-1]):
+        for far, other in PEERS if c < 2 else PEERS[::-1]:
             there = place(far, other)
-            slot = slot_of(far, other)
-            leaving[c].append(
-                pltpu.make_async_remote_copy(
-                    src_ref=made.at[c, :, pl.ds(pl.multiple_of(there * ROWS, ROWS), ROWS), :],
-                    dst_ref=spanned.at[c, :, :, pl.ds(pl.multiple_of(pos * LANES, LANES), LANES)],
-                    send_sem=out_send.at[c, slot],
-                    recv_sem=out_recv.at[c, slot],
-                    device_id=(base + there,),
-                    device_id_type=MESH,
-                )
-            )
-            leaving[c][-1].start()
+            pltpu.make_async_remote_copy(
+                src_ref=made.at[c, :, pl.ds(pl.multiple_of(there * ROWS, ROWS), ROWS), :],
+                dst_ref=spanned.at[c, :, :, pl.ds(pl.multiple_of(pos * LANES, LANES), LANES)],
+                send_sem=out_send,
+                recv_sem=out_recv.at[c] if c < 2 else last_recv.at[far % 8],
+                device_id=(base + there,),
+                device_id_type=MESH,
+            ).start()
 
     for c in range(3):
-        for index, far in enumerate((0, 1, -1, 2, -2, 3, -3, 4) if c < 2 else (4, -3, 3, -2, 2, -1, 1, 0)):
-            for copy, peer in zip(leaving[c], PEERS if c < 2 else PEERS[::-1]):
-                if peer[0] == far:
-                    copy.wait_recv()
+        if c < 2:
+            wait_for(spanned.at[c, :, :, pl.ds(0, 15 * LANES)], out_recv.at[c])
+        for index, far in enumerate((4, -3, 3, -2, 2, -1, 1, 0)):
+            if c == 2:
+                wait_for(spanned.at[c, :, :, pl.ds(0, 2 * LANES if far else LANES)], last_recv.at[far % 8])
             origin = pl.multiple_of(lax.rem(chip - far + 8, 8) * 256, 256)
             piece = spanned[c, :, :, pl.ds(origin, 256)].reshape(4 * ROWS, 256)
             term = jnp.dot(piece, turned[pl.ds(origin, 256), :], preferred_element_type=jnp.float32)
@@ -212,9 +238,9 @@
                     mixed[tile].reshape(ROWS, 4, LANES).astype(jnp.bfloat16)
                 )
 
-    for c in range(3):
-        for copy in arriving[c] + halos[c] + leaving[c]:
-            copy.wait_send()
+    wait_for(x.at[:, :, :, pl.ds(0, 15 * LANES)], in_send)
+    wait_for(held.at[:, pl.ds(0, GROUP)], halo_send)
+    wait_for(made.at[:, :, pl.ds(0, 15 * ROWS), :], out_send)
 
 
 def finish(moving, shown, velocity, final, sems):
@@ -258,14 +284,17 @@
             pltpu.VMEM((1, width), f32),
             pltpu.VMEM((3, width), f32),
             pltpu.VMEM((3, width), f32),
-            pltpu.SemaphoreType.DMA((3, 16)),
-            pltpu.SemaphoreType.DMA((3, 16)),
-            pltpu.SemaphoreType.DMA((3, 2)),
-            pltpu.SemaphoreType.DMA((3, 2)),
-            pltpu.SemaphoreType.DMA((3, 16)),
-            pltpu.SemaphoreType.DMA((3, 16)),
+            pltpu.SemaphoreType.DMA,
+            pltpu.SemaphoreType.DMA((3,)),
+            pltpu.SemaphoreType.DMA,
+            pltpu.SemaphoreType.DMA((3,)),
+            pltpu.SemaphoreType.DMA,
+            pltpu.SemaphoreType.DMA((2,)),
+            pltpu.SemaphoreType.DMA((8,)),
             pltpu.SemaphoreType.DMA((7,)),
-            pltpu.SemaphoreType.DMA((3,)),
+            pltpu.SemaphoreType.REGULAR((3,)),
+            pltpu.SemaphoreType.REGULAR,
+            pltpu.SemaphoreType.REGULAR,
         ],
         compiler_params=pltpu.CompilerParams(collective_id=0, has_side_effects=True, vmem_limit_bytes=60 * 2**20),
         name="inflow",

time: 84.9 us -> 80.4 us (0.947)
  Pallas kernels: 84.2 us -> 79.2 us
    pallas_call x1, Pallas kernels: 82.7 us -> 77.7 us  [body(): pl.pallas_call(kernel, out_shape=(pltpu.VMEM((parts, rows, planes, width)...]
where the time goes in v3:
time: 80.4 us; the launch traced here: 79.8 us
  Pallas kernels  79.2 us (99%)
    pallas_call x1, Pallas kernels, body(): pl.pallas_call(kernel, out_shape=(pltpu.VMEM((parts, rows, planes, width)...  77.7 us

profile of v3, /device:TPU:1, one launch (start us, length us, event | category | flops | bytes accessed | tf_op | source)
XLA Modules:
  0.0 79.8 jit_solution(1413237604993731327)
XLA Ops:
  0.6 77.7 %inflow.1 = (bf16[3,32,4,2048]{3,2,1,0:T(4,128)(2,1)S(1)}, f32[3,32,2048]{2,1,0:T(8,128)S(1)}) custom-call(bf16[32,3,4,2048]{3,2,1,0:T(4,128)(2,1)} %bitcast.5, bf16[2048,2048]{1,0:T(8,128)(2,1)} %wall.1, f32[3,32,2048]{2,1,0:T(8,128)} %bitcast.6, f32[513]{0:T(1024)} %weights.1, f32[3,2048]{1,0:T(4,128)} %scale.1, f32[1,2048]{1,0:T(1,128)} %bitcast.7, ...), custom_call_target="tpu_custom_call" | custom-call | tf_op jit(solution)/shard_map/inflow/pallas_call | solution.py:261
  78.3 1.4 %finish.1 = (bf16[32,3,4,2048]{3,2,1,0:T(4,128)(2,1)}, f32[3,32,2048]{2,1,0:T(8,128)}) custom-call(bf16[3,32,4,2048]{3,2,1,0:T(4,128)(2,1)S(1)} %get-tuple-element.6.moving, f32[3,32,2048]{2,1,0:T(8,128)S(1)} %get-tuple-element.7.shown), custom_call_target="tpu_custom_call" | custom-call | tf_op jit(solution)/shard_map/finish/pallas_call | solution.py:311

commit v4 on v3

--- a/solution.py
+++ b/solution.py
@@ -13,8 +13,13 @@
 PEERS = [(0, 1)] + [(sign * far, other) for far in (1, 2, 3) for sign in (1, -1) for other in (0, 1)] + [(4, 0), (4, 1)]
 
 
-NEAR = PEERS[:5]
-SCOUT = 8
+FARS = (1, -1, 2, -2, 3, -3, 4)
+ORDER = (0, 1, 2, 3, 7, 4, 6, 5)
+SCOUT = 0
+
+
+def rank(chip):
+    return jnp.minimum(2 * chip, 22 - 2 * chip) + jnp.where(chip == 5, 1, 0)
 
 
 def wait_for(view, sem):
@@ -26,7 +31,7 @@
     moving, shown,
     held, spread, columns, made, spanned, wide, turned, band, state, carried, sums, mixed,
     vweights, vscale, vmean, vdiag, voff,
-    in_send, in_recv, halo_send, halo_recv, out_send, out_recv, last_recv, load_sem, chain, scouts, release,
+    in_send, in_recv, halo_send, halo_recv, out_send, out_recv, last_recv, load_sem, ready, scouts, release,
 ):
     devices = lax.axis_size("span")
     me = lax.axis_index("span")
@@ -43,8 +48,19 @@
 
     scout = pos == SCOUT
     barrier = pltpu.get_barrier_semaphore()
-    for far, other in NEAR:
-        pl.semaphore_signal(barrier, inc=1, device_id=(base + place(far, other),), device_id_type=MESH)
+    mine = rank(chip)
+    ranks = {far: rank(lax.rem(chip + far + 8, 8)) for far in FARS}
+
+    def signal_chip(far, sem):
+        for other in (0, 1):
+            pl.semaphore_signal(sem, inc=1, device_id=(base + place(far, other),), device_id_type=MESH)
+
+    pl.semaphore_signal(barrier, inc=1, device_id=(base + place(0, 1),), device_id_type=MESH)
+    for far in FARS:
+
+        @pl.when(ranks[far] > mine)
+        def _():
+            signal_chip(far, barrier)
 
     @pl.when(scout)
     def _():
@@ -73,30 +89,38 @@
             device_id_type=MESH,
         ).start()
 
-    @pl.when(scout)
-    def _():
-        pl.semaphore_wait(barrier, len(NEAR) + 2)
-
-    @pl.when(jnp.logical_not(scout))
-    def _():
-        pl.semaphore_wait(barrier, len(NEAR))
-
-    for far, other in NEAR:
-        send_in(0, far, other)
-    for stage, reach in enumerate(((2, -2), (3, -3), (4,))):
-
-        @pl.when(core == 1)
+    for level, greeted in ((0, 0), (2, 1), (4, 2), (6, 3), (8, 4), (10, 6), (11, 7)):
+
+        @pl.when(mine == level)
         def _():
-            for sign in (1, -1):
-                for other in (0, 1):
-                    pl.semaphore_signal(
-                        chain.at[stage], inc=1, device_id=(base + place(sign, other),), device_id_type=MESH
-                    )
-
-        pl.semaphore_wait(chain.at[stage], 2)
-        for far in reach:
-            for other in (0, 1):
-                send_in(0, far, other)
+            if level == 0:
+
+                @pl.when(scout)
+                def _():
+                    pl.semaphore_wait(barrier, 3)
+
+                @pl.when(jnp.logical_not(scout))
+                def _():
+                    pl.semaphore_wait(barrier, 1)
+
+            else:
+                pl.semaphore_wait(barrier, 2 * greeted + 1)
+
+    for far in FARS:
+
+        @pl.when(ranks[far] < mine)
+        def _():
+            signal_chip(far, ready.at[chip])
+
+    send_in(0, 0, 1)
+    for far in FARS:
+
+        @pl.when(ranks[far] > mine)
+        def _():
+            pl.semaphore_wait(ready.at[lax.rem(chip + far + 8, 8)], 2)
+
+        for other in (0, 1):
+            send_in(0, far, other)
     for c in (1, 2):
         for far, other in PEERS:
             send_in(c, far, other)
@@ -189,21 +213,31 @@
         spanned[c, :, :, pl.ds(pl.multiple_of(pos * LANES, LANES), LANES)] = made[
             c, :, pl.ds(pl.multiple_of(pos * ROWS, ROWS), ROWS), :
         ]
-        for far, other in PEERS if c < 2 else PEERS[::-1]:
-            there = place(far, other)
+        def send_out(there, sem):
             pltpu.make_async_remote_copy(
                 src_ref=made.at[c, :, pl.ds(pl.multiple_of(there * ROWS, ROWS), ROWS), :],
                 dst_ref=spanned.at[c, :, :, pl.ds(pl.multiple_of(pos * LANES, LANES), LANES)],
                 send_sem=out_send,
-                recv_sem=out_recv.at[c] if c < 2 else last_recv.at[far % 8],
+                recv_sem=sem,
                 device_id=(base + there,),
                 device_id_type=MESH,
             ).start()
 
+        if c < 2:
+            for far, other in PEERS:
+                send_out(place(far, other), out_recv.at[c])
+        else:
+            for target in ORDER:
+                for side in (0, 1):
+
+                    @pl.when(pos != 2 * target + side)
+                    def _():
+                        send_out(2 * target + side, last_recv.at[lax.rem(target - chip + 8, 8)])
+
     for c in range(3):
         if c < 2:
             wait_for(spanned.at[c, :, :, pl.ds(0, 15 * LANES)], out_recv.at[c])
-        for index, far in enumerate((4, -3, 3, -2, 2, -1, 1, 0)):
+        for index, far in enumerate((0, 1, -1, 2, -2, 3, -3, 4)):
             if c == 2:
                 wait_for(spanned.at[c, :, :, pl.ds(0, 2 * LANES if far else LANES)], last_recv.at[far % 8])
             origin = pl.multiple_of(lax.rem(chip - far + 8, 8) * 256, 256)
@@ -292,7 +326,7 @@
             pltpu.SemaphoreType.DMA((2,)),
             pltpu.SemaphoreType.DMA((8,)),
             pltpu.SemaphoreType.DMA((7,)),
-            pltpu.SemaphoreType.REGULAR((3,)),
+            pltpu.SemaphoreType.REGULAR((8,)),
             pltpu.SemaphoreType.REGULAR,
             pltpu.SemaphoreType.REGULAR,
         ],

time: 80.4 us -> 78.8 us (0.980)
  Pallas kernels: 79.2 us -> 77.4 us
    pallas_call x1, Pallas kernels: 77.7 us -> 76 us  [body(): pl.pallas_call(kernel, out_shape=(pltpu.VMEM((parts, rows, planes, width)...]
where the time goes in v4:
time: 78.8 us; the launch traced here: 78.1 us
  Pallas kernels  77.4 us (98%)
    pallas_call x1, Pallas kernels, body(): pl.pallas_call(kernel, out_shape=(pltpu.VMEM((parts, rows, planes, width)...  76 us

profile of v4, /device:TPU:1, one launch (start us, length us, event | category | flops | bytes accessed | tf_op | source)
XLA Modules:
  0.0 78.1 jit_solution(8865450397481197543)
XLA Ops:
  0.6 76.0 %inflow.1 = (bf16[3,32,4,2048]{3,2,1,0:T(4,128)(2,1)S(1)}, f32[3,32,2048]{2,1,0:T(8,128)S(1)}) custom-call(bf16[32,3,4,2048]{3,2,1,0:T(4,128)(2,1)} %bitcast.5, bf16[2048,2048]{1,0:T(8,128)(2,1)} %wall.1, f32[3,32,2048]{2,1,0:T(8,128)} %bitcast.6, f32[513]{0:T(1024)} %weights.1, f32[3,2048]{1,0:T(4,128)} %scale.1, f32[1,2048]{1,0:T(1,128)} %bitcast.7, ...), custom_call_target="tpu_custom_call" | custom-call | tf_op jit(solution)/shard_map/inflow/pallas_call | solution.py:295
  76.6 1.4 %finish.1 = (bf16[32,3,4,2048]{3,2,1,0:T(4,128)(2,1)}, f32[3,32,2048]{2,1,0:T(8,128)}) custom-call(bf16[3,32,4,2048]{3,2,1,0:T(4,128)(2,1)S(1)} %get-tuple-element.6.moving, f32[3,32,2048]{2,1,0:T(8,128)S(1)} %get-tuple-element.7.shown), custom_call_target="tpu_custom_call" | custom-call | tf_op jit(solution)/shard_map/finish/pallas_call | solution.py:345

commit v5 on v4

--- a/solution.py
+++ b/solution.py
@@ -13,13 +13,22 @@
 PEERS = [(0, 1)] + [(sign * far, other) for far in (1, 2, 3) for sign in (1, -1) for other in (0, 1)] + [(4, 0), (4, 1)]
 
 
-FARS = (1, -1, 2, -2, 3, -3, 4)
 ORDER = (0, 1, 2, 3, 7, 4, 6, 5)
 SCOUT = 0
 
 
-def rank(chip):
-    return jnp.minimum(2 * chip, 22 - 2 * chip) + jnp.where(chip == 5, 1, 0)
+EARLIER = {0: (), 1: (0,), 2: (0, 1), 3: (0, 1, 2), 4: (0, 1, 2, 3), 5: (0, 1, 2, 3, 4), 6: (0, 1, 4, 7), 7: (0, 1)}
+RELAY = 8
+ENTRY = {
+    0: (("wait", 1), 1, ("wait", 2), 2, ("wait", 7), 7, ("wait", 3), 3, ("wait", 6), 6, ("wait", 4), 4, ("wait", 5), 5),
+    1: (0, ("wait", 2), 2, ("wait", 3), 3, ("wait", 7), 7, ("wait", 4), 4, ("wait", 6), 6, ("wait", 5), 5),
+    2: (1, 0, ("wait", 3), 3, ("wait", 4), 4, ("wait", 5), 5, ("wait", RELAY), 6, 7),
+    3: (2, 1, 0, ("wait", 4), 4, ("wait", 5), 5, ("wait", RELAY), 6, 7),
+    4: (3, 2, 1, 0, ("wait", 5), ("wait", 6), ("relay", (5, 6, 3, 2)), 5, 6, 7),
+    5: (4, 3, 2, 1, 0, ("wait", RELAY), 6, 7),
+    6: (7, 4, 0, 1, ("wait", RELAY), ("relay", (7,)), 5, 2, 3),
+    7: (0, 1, ("wait", 6), 6, 4, ("wait", RELAY), 5, 2, 3),
+}
 
 
 def wait_for(view, sem):
@@ -48,19 +57,19 @@
 
     scout = pos == SCOUT
     barrier = pltpu.get_barrier_semaphore()
-    mine = rank(chip)
-    ranks = {far: rank(lax.rem(chip + far + 8, 8)) for far in FARS}
-
-    def signal_chip(far, sem):
-        for other in (0, 1):
-            pl.semaphore_signal(sem, inc=1, device_id=(base + place(far, other),), device_id_type=MESH)
+
+    def signal_chip(target, sem):
+        for side in (0, 1):
+            pl.semaphore_signal(sem, inc=1, device_id=(base + 2 * target + side,), device_id_type=MESH)
 
     pl.semaphore_signal(barrier, inc=1, device_id=(base + place(0, 1),), device_id_type=MESH)
-    for far in FARS:
-
-        @pl.when(ranks[far] > mine)
+    for which in range(8):
+
+        @pl.when(chip == which)
         def _():
-            signal_chip(far, barrier)
+            for target in ORDER:
+                if which in EARLIER[target]:
+                    signal_chip(target, barrier)
 
     @pl.when(scout)
     def _():
@@ -78,8 +87,7 @@
             x.at[:, c, :, pl.ds(pl.multiple_of(pos * LANES, LANES), LANES)], held.at[c, 8 + pos], in_recv.at[c]
         ).start()
 
-    def send_in(c, far, other):
-        there = place(far, other)
+    def send_in(c, there):
         pltpu.make_async_remote_copy(
             src_ref=x.at[:, c, :, pl.ds(pl.multiple_of(there * LANES, LANES), LANES)],
             dst_ref=held.at[c, 8 + pos],
@@ -89,41 +97,34 @@
             device_id_type=MESH,
         ).start()
 
-    for level, greeted in ((0, 0), (2, 1), (4, 2), (6, 3), (8, 4), (10, 6), (11, 7)):
-
-        @pl.when(mine == level)
+    @pl.when(scout)
+    def _():
+        pl.semaphore_wait(barrier, 3)
+
+    for which in range(8):
+
+        @pl.when(jnp.logical_and(chip == which, jnp.logical_not(scout)))
         def _():
-            if level == 0:
-
-                @pl.when(scout)
-                def _():
-                    pl.semaphore_wait(barrier, 3)
-
-                @pl.when(jnp.logical_not(scout))
-                def _():
-                    pl.semaphore_wait(barrier, 1)
-
-            else:
-                pl.semaphore_wait(barrier, 2 * greeted + 1)
-
-    for far in FARS:
-
-        @pl.when(ranks[far] < mine)
+            pl.semaphore_wait(barrier, 2 * len(EARLIER[which]) + 1)
+
+        @pl.when(chip == which)
         def _():
-            signal_chip(far, ready.at[chip])
-
-    send_in(0, 0, 1)
-    for far in FARS:
-
-        @pl.when(ranks[far] > mine)
-        def _():
-            pl.semaphore_wait(ready.at[lax.rem(chip + far + 8, 8)], 2)
-
-        for other in (0, 1):
-            send_in(0, far, other)
+            for target in EARLIER[which]:
+                signal_chip(target, ready.at[which])
+            send_in(0, place(0, 1))
+            for step in ENTRY[which]:
+                if isinstance(step, int):
+                    send_in(0, 2 * step)
+                    send_in(0, 2 * step + 1)
+                elif step[0] == "wait":
+                    pl.semaphore_wait(ready.at[step[1]], 2)
+                else:
+                    for target in step[1]:
+                        signal_chip(target, ready.at[RELAY])
+
     for c in (1, 2):
         for far, other in PEERS:
-            send_in(c, far, other)
+            send_in(c, place(far, other))
 
     @pl.when(scout)
     def _():
@@ -326,7 +327,7 @@
             pltpu.SemaphoreType.DMA((2,)),
             pltpu.SemaphoreType.DMA((8,)),
             pltpu.SemaphoreType.DMA((7,)),
-            pltpu.SemaphoreType.REGULAR((8,)),
+            pltpu.SemaphoreType.REGULAR((9,)),
             pltpu.SemaphoreType.REGULAR,
             pltpu.SemaphoreType.REGULAR,
         ],

time: 78.8 us -> 77.6 us (0.985)
  no operation moved by 1% of the time
where the time goes in v5:
time: 77.6 us; the launch traced here: 77.5 us
  Pallas kernels  76.9 us (99%)
    pallas_call x1, Pallas kernels, body(): pl.pallas_call(kernel, out_shape=(pltpu.VMEM((parts, rows, planes, width)...  75.4 us

profile of v5, /device:TPU:1, one launch (start us, length us, event | category | flops | bytes accessed | tf_op | source)
XLA Modules:
  0.0 77.5 jit_solution(6043048188452843278)
XLA Ops:
  0.6 75.4 %inflow.1 = (bf16[3,32,4,2048]{3,2,1,0:T(4,128)(2,1)S(1)}, f32[3,32,2048]{2,1,0:T(8,128)S(1)}) custom-call(bf16[32,3,4,2048]{3,2,1,0:T(4,128)(2,1)} %bitcast.5, bf16[2048,2048]{1,0:T(8,128)(2,1)} %wall.1, f32[3,32,2048]{2,1,0:T(8,128)} %bitcast.6, f32[513]{0:T(1024)} %weights.1, f32[3,2048]{1,0:T(4,128)} %scale.1, f32[1,2048]{1,0:T(1,128)} %bitcast.7, ...), custom_call_target="tpu_custom_call" | custom-call | tf_op jit(solution)/shard_map/inflow/pallas_call | solution.py:296
  76.0 1.4 %finish.1 = (bf16[32,3,4,2048]{3,2,1,0:T(4,128)(2,1)}, f32[3,32,2048]{2,1,0:T(8,128)}) custom-call(bf16[3,32,4,2048]{3,2,1,0:T(4,128)(2,1)S(1)} %get-tuple-element.6.moving, f32[3,32,2048]{2,1,0:T(8,128)S(1)} %get-tuple-element.7.shown), custom_call_target="tpu_custom_call" | custom-call | tf_op jit(solution)/shard_map/finish/pallas_call | solution.py:346

commit v6 on v5

--- a/solution.py
+++ b/solution.py
@@ -17,17 +17,17 @@
 SCOUT = 0
 
 
-EARLIER = {0: (), 1: (0,), 2: (0, 1), 3: (0, 1, 2), 4: (0, 1, 2, 3), 5: (0, 1, 2, 3, 4), 6: (0, 1, 4, 7), 7: (0, 1)}
+EARLIER = {0: (), 1: (0,), 2: (0, 1), 3: (0, 1, 2), 4: (0, 1, 2, 3), 5: (0, 1, 2, 3, 4, 6), 6: (0, 1, 4, 7), 7: (0, 1)}
 RELAY = 8
 ENTRY = {
     0: (("wait", 1), 1, ("wait", 2), 2, ("wait", 7), 7, ("wait", 3), 3, ("wait", 6), 6, ("wait", 4), 4, ("wait", 5), 5),
     1: (0, ("wait", 2), 2, ("wait", 3), 3, ("wait", 7), 7, ("wait", 4), 4, ("wait", 6), 6, ("wait", 5), 5),
     2: (1, 0, ("wait", 3), 3, ("wait", 4), 4, ("wait", 5), 5, ("wait", RELAY), 6, 7),
     3: (2, 1, 0, ("wait", 4), 4, ("wait", 5), 5, ("wait", RELAY), 6, 7),
-    4: (3, 2, 1, 0, ("wait", 5), ("wait", 6), ("relay", (5, 6, 3, 2)), 5, 6, 7),
-    5: (4, 3, 2, 1, 0, ("wait", RELAY), 6, 7),
-    6: (7, 4, 0, 1, ("wait", RELAY), ("relay", (7,)), 5, 2, 3),
-    7: (0, 1, ("wait", 6), 6, 4, ("wait", RELAY), 5, 2, 3),
+    4: (3, 2, 1, 0, ("wait", 5), ("wait", 6), ("relay", (5, 3, 2)), 5, 6, 7),
+    5: (6, 4, 3, 2, 1, 0, ("wait", RELAY), 7),
+    6: (7, 4, 0, 1, ("fill", (7, 4)), ("wait", 5), ("relay", (7,)), 5, 2, 3),
+    7: (0, 1, ("fill", (0, 1)), ("wait", 6), 6, 4, ("wait", RELAY), 5, 2, 3),
 }
 
 
@@ -112,19 +112,27 @@
             for target in EARLIER[which]:
                 signal_chip(target, ready.at[which])
             send_in(0, place(0, 1))
+            early = set()
             for step in ENTRY[which]:
                 if isinstance(step, int):
                     send_in(0, 2 * step)
                     send_in(0, 2 * step + 1)
                 elif step[0] == "wait":
                     pl.semaphore_wait(ready.at[step[1]], 2)
+                elif step[0] == "relay":
+                    for target in step[1]:
+                        signal_chip(target, ready.at[RELAY])
                 else:
                     for target in step[1]:
-                        signal_chip(target, ready.at[RELAY])
-
-    for c in (1, 2):
-        for far, other in PEERS:
-            send_in(c, place(far, other))
+                        send_in(1, 2 * target)
+                        send_in(1, 2 * target + 1)
+                        early.add(target)
+            for far, other in PEERS:
+                if (which + far) % 8 not in early:
+                    send_in(1, place(far, other))
+
+    for far, other in PEERS:
+        send_in(2, place(far, other))
 
     @pl.when(scout)
     def _():

time: 77.6 us -> 77.6 us (level)
  no operation moved by 1% of the time
where the time goes in v6:
time: 77.6 us; the launch traced here: 77.5 us
  Pallas kernels  76.9 us (99%)
    pallas_call x1, Pallas kernels, body(): pl.pallas_call(kernel, out_shape=(pltpu.VMEM((parts, rows, planes, width)...  75.4 us

profile of v6, /device:TPU:1, one launch (start us, length us, event | category | flops | bytes accessed | tf_op | source)
XLA Modules:
  0.0 77.5 jit_solution(10273655151949332062)
XLA Ops:
  0.6 75.4 %inflow.1 = (bf16[3,32,4,2048]{3,2,1,0:T(4,128)(2,1)S(1)}, f32[3,32,2048]{2,1,0:T(8,128)S(1)}) custom-call(bf16[32,3,4,2048]{3,2,1,0:T(4,128)(2,1)} %bitcast.5, bf16[2048,2048]{1,0:T(8,128)(2,1)} %wall.1, f32[3,32,2048]{2,1,0:T(8,128)} %bitcast.6, f32[513]{0:T(1024)} %weights.1, f32[3,2048]{1,0:T(4,128)} %scale.1, f32[1,2048]{1,0:T(1,128)} %bitcast.7, ...), custom_call_target="tpu_custom_call" | custom-call | tf_op jit(solution)/shard_map/inflow/pallas_call | solution.py:304
  76.1 1.4 %finish.1 = (bf16[32,3,4,2048]{3,2,1,0:T(4,128)(2,1)}, f32[3,32,2048]{2,1,0:T(8,128)}) custom-call(bf16[3,32,4,2048]{3,2,1,0:T(4,128)(2,1)S(1)} %get-tuple-element.6.moving, f32[3,32,2048]{2,1,0:T(8,128)S(1)} %get-tuple-element.7.shown), custom_call_target="tpu_custom_call" | custom-call | tf_op jit(solution)/shard_map/finish/pallas_call | solution.py:354
